TPU v7x, 32 devices: a whole 2x2x4 slice. The times are simulated.
32 devices in a mesh: dp: 8 (over z, y), query: 4 (over x, core).
Axes of the slice: x: 2, y: 2, z: 4, core: 2. Of those that a mesh axis runs over, the one named last changes fastest.
Arguments:
- sensors: bfloat16 [3072, 4096], P('dp'), may hold values from -8 to 8
- query_index: int32 [2, 8192], P(None, 'query'), may hold values from 0 to 127
- targets: bfloat16 [3072, 8192], P('dp', 'query'), may hold values from -6 to 6
- w_one: bfloat16 [4096, 1024], P(None, 'query'), may hold values from -0.09375 to 0.09375
- b_one: float32 [1024], P('query'), may hold values from -3 to 3
- w_two: bfloat16 [1024, 512], P('query'), may hold values from -0.1875 to 0.1875
- b_two: float32 [512], replicated, may hold values from -3 to 3
- v_one: float32 [2, 512], replicated, may hold values from -4 to 4
- c_one: float32 [512], replicated, may hold values from -3 to 3
- v_two: bfloat16 [512, 512], replicated, may hold values from -0.25 to 0.25
- c_two: float32 [512], replicated, may hold values from -3 to 3
- v_three: bfloat16 [512, 512], replicated, may hold values from -0.25 to 0.25
- c_three: float32 [512], replicated, may hold values from -3 to 3
Outputs:
- loss: float32 [], replicated
- grad_w_one: float32 [4096, 1024], P('dp', 'query')
- grad_b_one: float32 [1024], P('query')
- grad_w_two: float32 [1024, 512], P('query', 'dp')
- grad_b_two: float32 [512], replicated
- grad_v_one: float32 [2, 512], replicated
- grad_c_one: float32 [512], replicated
- grad_v_two: float32 [512, 512], replicated
- grad_c_two: float32 [512], replicated
- grad_v_three: float32 [512, 512], replicated
- grad_c_three: float32 [512], replicated
All inputs are finite; a program needn't handle non-finite values.
Results may differ from a plain program's by a relative error of at most 0.00075.
Values may be sent and summed in bfloat16 or wider, within the bound.
A program may use at most 128 MiB of HBM per device.

v0:
```python
import math
import jax
import jax.numpy as jnp
from jax import lax
from jax.sharding import PartitionSpec as P

GRID = 128


def contract_rows(left, right, precision=None):
    return lax.dot_general(
        left,
        right,
        (((0,), (0,)), ((), ())),
        precision=precision,
        preferred_element_type=jnp.float32,
    )


def contract_cols(left, right, precision=None):
    return lax.dot_general(
        left,
        right,
        (((1,), (1,)), ((), ())),
        precision=precision,
        preferred_element_type=jnp.float32,
    )


def trunk_forward(coords, v_one, c_one, v_two, c_two, v_three, c_three):
    first_act = jnp.tanh(
        coords[0][:, None] * v_one[0][None, :] + coords[1][:, None] * v_one[1][None, :] + c_one
    )
    first_b = first_act.astype(jnp.bfloat16)
    second_act = jnp.tanh(jnp.dot(first_b, v_two, preferred_element_type=jnp.float32) + c_two)
    second_b = second_act.astype(jnp.bfloat16)
    basis_full = jnp.dot(second_b, v_three, preferred_element_type=jnp.float32) + c_three
    return (first_act, first_b, second_act, second_b, basis_full.astype(jnp.bfloat16))


def trunk_backward(coords, first_act, first_b, second_act, second_b, grad_basis, v_two, v_three):
    grad_basis_b = grad_basis.astype(jnp.bfloat16)
    grad_v_three = contract_rows(second_b, grad_basis_b)
    grad_c_three = jnp.sum(grad_basis, axis=0)
    grad_second = contract_cols(grad_basis_b, v_three) * (1.0 - second_act * second_act)
    grad_second_b = grad_second.astype(jnp.bfloat16)
    grad_v_two = contract_rows(first_b, grad_second_b)
    grad_c_two = jnp.sum(grad_second, axis=0)
    grad_first = contract_cols(grad_second_b, v_two) * (1.0 - first_act * first_act)
    grad_v_one = jnp.dot(
        coords, grad_first, precision=lax.Precision.HIGHEST, preferred_element_type=jnp.float32
    )
    grad_c_one = jnp.sum(grad_first, axis=0)
    return (grad_v_one, grad_c_one, grad_v_two, grad_c_two, grad_v_three, grad_c_three)


def local(
    sensors,
    query_index,
    targets,
    w_one,
    b_one,
    w_two,
    b_two,
    v_one,
    c_one,
    v_two,
    c_two,
    v_three,
    c_three,
):
    dp_count = lax.axis_size("dp")
    func_rows = sensors.shape[0]
    query_rows = query_index.shape[1]
    count_all = func_rows * dp_count * query_rows * lax.axis_size("query")
    grad_scale = 64.0 / math.sqrt(count_all)
    inv_scale = 1.0 / math.sqrt(w_two.shape[1])
    coords_all = query_index.astype(jnp.float32) / (GRID - 1)
    hidden = jnp.tanh(jnp.dot(sensors, w_one, preferred_element_type=jnp.float32) + b_one)
    hidden_b = hidden.astype(jnp.bfloat16)
    partial_value = jnp.dot(hidden_b, w_two, preferred_element_type=jnp.float32)
    coeffs = lax.psum(partial_value, "query") + b_two
    coeffs_b = coeffs.astype(jnp.bfloat16)
    row_share = query_rows // dp_count
    coords_mine = lax.dynamic_slice_in_dim(
        coords_all, lax.axis_index("dp") * row_share, row_share, 1
    )
    first_act, first_b, second_act, second_b, basis_b = trunk_forward(
        coords_mine, v_one, c_one, v_two, c_two, v_three, c_three
    )
    basis_all = lax.all_gather(basis_b, "dp", axis=0, tiled=True)
    prediction = contract_cols(coeffs_b, basis_all) * inv_scale
    misfit = prediction - targets.astype(jnp.float32)
    loss_part = jnp.sum(misfit * misfit)
    misfit_b = (misfit * grad_scale).astype(jnp.bfloat16)
    grad_coeffs = lax.psum(
        jnp.dot(misfit_b, basis_all, preferred_element_type=jnp.float32) * inv_scale, "query"
    )
    grad_coeffs_b = grad_coeffs.astype(jnp.bfloat16)
    loss_value = lax.psum(loss_part, ("dp", "query")) / count_all
    columns = misfit_b
    grad_basis = lax.psum_scatter(
        contract_rows(columns, coeffs_b) * inv_scale, "dp", scatter_dimension=0, tiled=True
    )
    trunk_parts = trunk_backward(
        coords_mine, first_act, first_b, second_act, second_b, grad_basis, v_two, v_three
    )
    grad_w_two_part = contract_rows(hidden_b, grad_coeffs_b)
    grad_pre = contract_cols(grad_coeffs_b, w_two) * (1.0 - hidden * hidden)
    grad_pre_b = grad_pre.astype(jnp.bfloat16)
    grad_b_one, grad_b_two = lax.psum(
        (jnp.sum(grad_pre, axis=0), jnp.sum(grad_coeffs, axis=0)), "dp"
    )
    columns = sensors
    grad_w_one = lax.psum_scatter(
        contract_rows(columns, grad_pre_b), "dp", scatter_dimension=0, tiled=True
    )
    grad_w_two = lax.psum_scatter(grad_w_two_part, "dp", scatter_dimension=1, tiled=True)
    trunk_sums = lax.psum(
        (
            trunk_parts[0],
            trunk_parts[1],
            trunk_parts[2],
            trunk_parts[3],
            trunk_parts[4],
            trunk_parts[5],
        ),
        ("dp", "query"),
    )
    return (
        loss_value,
        grad_w_one,
        grad_b_one,
        grad_w_two,
        grad_b_two,
        trunk_sums[0],
        trunk_sums[1],
        trunk_sums[2],
        trunk_sums[3],
        trunk_sums[4],
        trunk_sums[5],
    )


def solution(mesh):
    placed = (
        P("dp", None),
        P(None, "query"),
        P("dp", "query"),
        P(None, "query"),
        P("query"),
        P("query", None),
        P(),
        P(),
        P(),
        P(),
        P(),
        P(),
        P(),
    )
    return jax.shard_map(
        local,
        mesh=mesh,
        in_specs=placed,
        out_specs=(
            P(),
            P("dp", "query"),
            P("query"),
            P("query", "dp"),
            P(),
            P(),
            P(),
            P(),
            P(),
            P(),
            P(),
        ),
        check_vma=False,
    )
```

profile of v0, /device:TPU:0, one launch (start us, length us, event | category | flops | bytes accessed | tf_op | source)
XLA Modules:
  0.0 356.2 jit_solution(2929589968027508688)
XLA Ops:
  8.1 1.8 copy-done
  9.9 2.6 fusion.2
  12.6 1.1 fusion.19
  14.5 0.8 fusion.24
  15.3 1.4 fusion
  16.7 0.8 copy-done.2
  17.5 2.1 fusion.1
  19.6 32.0 %all-reduce.7.cloned.1.call-done = f32[384,512]{1,0:T(8,128)} async-done(((f32[384,512]{1,0:T(8,128)}), f32[384,512]{1,0:T(8,128)}) %all-reduce.7.cloned.1.call-update) | async-done | bytes 786448 | tf_op jit(solution)/shard_map/psum | solution.py:82
  51.6 19.8 %all-gather.2.cloned.1.call-done = bf16[2048,512]{1,0:T(8,128)(2,1)} async-done(((bf16[256,512]{1,0:T(8,128)(2,1)}), bf16[2048,512]{1,0:T(8,128)(2,1)}) %all-gather.2.cloned.1.call-update) | async-done | bytes 2097168 | tf_op jit(solution)/shard_map/all_gather | solution.py:91
  71.4 4.2 %multiply_reduce_fusion = (f32[]{:T(128)}, f32[384,2048]{1,0:T(8,128)S(1)}) fusion(bf16[384,2048]{1,0:T(8,128)(2,1)} %param.15, bf16[2048,512]{1,0:T(8,128)(2,1)} %all-gather.2.cloned.1.call-done, f32[384,512]{1,0:T(8,128)} %all-reduce.7.cloned.1.call-done, f32[512]{0:T(512)S(1)} %copy-done.7), kind=kOutput, calls=%fused_computation.3 | convolution fusion | flops 809631744 | bytes 7604228 | tf_op jit(solution)/shard_map/dot_general | solution.py:21
  75.6 1.6 copy-done.1
  77.2 1.9 convolution_multiply_fusion.1
  79.2 5.3 %convolution_multiply_fusion = f32[2048,512]{1,0:T(8,128)} fusion(f32[384,2048]{1,0:T(8,128)} %copy-done.1, f32[384,512]{1,0:T(8,128)} %all-reduce.7.cloned.1.call-done, f32[512]{0:T(512)S(1)} %copy-done.7), kind=kOutput, calls=%fused_computation.1 | convolution fusion | flops 808321024 | bytes 8128512 | tf_op jit(solution)/shard_map/dot_general | solution.py:11
  84.6 28.1 %all-reduce.9.cloned.1.call-done = f32[384,512]{1,0:T(8,128)} async-done(((f32[384,512]{1,0:T(8,128)}), f32[384,512]{1,0:T(8,128)}) %all-reduce.9.cloned.1.call-update) | async-done | bytes 786448 | tf_op jit(solution)/shard_map/psum | solution.py:96
  112.8 2.1 fusion.28
  114.8 3.2 convolution_bitcast_fusion
  118.1 2.3 fusion.8
  120.5 51.0 %reduce-scatter.8.cloned.1.call-done = f32[256,512]{1,0:T(8,128)} async-done(((f32[2048,512]{1,0:T(8,128)}), f32[256,512]{1,0:T(8,128)}) %reduce-scatter.8.cloned.1.call-update) | async-done | bytes 524304 | tf_op jit(solution)/shard_map/reduce_scatter | solution.py:102
  171.5 1.8 fusion.27
  173.3 2.2 fusion.4
  175.5 1.3 fusion.13
  176.8 1.2 reduce_sum.56
  178.0 21.5 %all-reduce.2 = (f32[256]{0:T(256)}, f32[512]{0:T(512)}) all-reduce(f32[256]{0:T(256)S(1)} %copy-done.12, f32[512]{0:T(512)S(1)} %reduce_sum.56), channel_id=1, replica_groups=mesh['dp'=8,'query'=4] {'dp'}, use_global_device_ids=true, to_apply=%region_6.0 | all-reduce | flops 768 | bytes 6144 | tf_op jit(solution)/shard_map/psum | solution.py:111
  199.6 1.1 reduce_sum.59
  200.7 1.4 fusion.26
  202.5 38.7 %all-reduce = (f32[]{:T(128)}, f32[2,512]{1,0:T(2,128)}, f32[512]{0:T(512)}, f32[512]{0:T(512)}, f32[512]{0:T(512)}) all-reduce(f32[]{:T(128)} %get-tuple-element.35, f32[2,512]{1,0:T(2,128)S(1)} %fusion.29, f32[512]{0:T(512)S(1)} %get-tuple-element.37, ...), channel_id=1, replica_groups=mesh['dp'=8,'query'=4] {'dp','query'}, use_global_device_ids=true, to_apply=%region_2.0 | all-reduce | flops 2561 | bytes 20488 | tf_op jit(solution)/shard_map/psum | solution.py:100
  241.8 31.0 %reduce-scatter.4.cloned.1.call-done = f32[512,256]{0,1:T(8,128)} async-done(((f32[4096,256]{0,1:T(8,128)}), f32[512,256]{0,1:T(8,128)}) %reduce-scatter.4.cloned.1.call-update) | async-done | bytes 524304 | tf_op jit(solution)/shard_map/reduce_scatter | solution.py:115
  272.8 2.0 copy.24
  274.8 64.7 %reduce-scatter.6.cloned.1.call-done = f32[256,64]{0,1:T(8,128)} async-done(((f32[256,512]{0,1:T(8,128)}), f32[256,64]{0,1:T(8,128)}) %reduce-scatter.6.cloned.1.call-update) | async-done | bytes 65552 | tf_op jit(solution)/shard_map/reduce_scatter | solution.py:118
  339.5 3.7 %all-reduce.11.cloned.1.call-done = (f32[512,512]{1,0:T(8,128)}, f32[512,512]{1,0:T(8,128)}) async-done(((f32[512,512]{1,0:T(8,128)}, f32[512,512]{1,0:T(8,128)}), (f32[512,512]{1,0:T(8,128)}, f32[512,512]{1,0:T(8,128)})) %all-reduce.11.cloned.1.call-update) | async-done | bytes 2097168 | tf_op jit(solution)/shard_map/psum | solution.py:119
  343.2 2.3 copy.29
  345.5 2.3 copy.30
  (42 shorter events, 1.5 us)
Async XLA Ops:
  8.0 1.9 copy-start
  8.0 43.6 %all-reduce.7.cloned.1.call-start = ((), (), s32[]{:S(2)}) async-start(), calls=%async_computation.3 | async-start | bytes 1572864 | tf_op jit(solution)/shard_map/psum | solution.py:82
  9.9 2.6 copy-start.6
  12.5 58.9 %copy-start.7 = (f32[512]{0:T(512)S(1)}, f32[512]{0:T(512)}, u32[]{:S(2)}) copy-start(f32[512]{0:T(512)} %param.19) | copy-start | bytes 6148
  13.7 57.7 %all-gather.2.cloned.1.call-start = ((), (), s32[]{:S(2)}) async-start(), calls=%async_computation.4 | async-start | bytes 2359296 | tf_op jit(solution)/shard_map/all_gather | solution.py:91
  14.5 0.8 copy-start.8
  14.5 2.2 copy-start.10
  16.7 0.8 copy-start.2
  19.6 93.2 %all-reduce.9.cloned.1.call-start = ((), (), s32[]{:S(2)}) async-start(), calls=%async_computation.5 | async-start | bytes 1572864 | tf_op jit(solution)/shard_map/psum | solution.py:96
  71.4 5.8 %copy-start.5 = (bf16[2048,512]{1,0:T(8,128)(2,1)S(1)}, bf16[2048,512]{1,0:T(8,128)(2,1)}, u32[]{:S(2)}) copy-start(bf16[2048,512]{1,0:T(8,128)(2,1)} %all-gather.2.cloned.1.call-done) | copy-start | bytes 6291460
  75.6 1.6 copy-start.1
  79.1 92.3 %reduce-scatter.8.cloned.1.call-start = ((), (), s32[]{:S(2)}) async-start(), calls=%async_computation.8 | async-start | bytes 4718592 | tf_op jit(solution)/shard_map/reduce_scatter | solution.py:102
  84.5 188.2 %reduce-scatter.4.cloned.1.call-start = ((), (), s32[]{:S(2)}) async-start(), calls=%async_computation.6 | async-start | bytes 4718592 | tf_op jit(solution)/shard_map/reduce_scatter | solution.py:115
  118.0 55.2 %copy-start.9 = (f32[1,256]{1,0:T(1,128)S(1)}, f32[1,256]{1,0:T(1,128)}, u32[]{:S(2)}) copy-start(f32[1,256]{1,0:T(1,128)} %copy-done.8) | copy-start | bytes 3076
  118.1 221.4 %reduce-scatter.6.cloned.1.call-start = ((), (), s32[]{:S(2)}) async-start(), calls=%async_computation.7 | async-start | bytes 589824 | tf_op jit(solution)/shard_map/reduce_scatter | solution.py:118
  120.4 222.8 %all-reduce.11.cloned.1.call-start = ((), (), s32[]{:S(2)}) async-start(), calls=%async_computation.9 | async-start | bytes 4194304 | tf_op jit(solution)/shard_map/psum | solution.py:119
  171.5 4.0 %copy-start.3 = (f32[256,512]{1,0:T(8,128)S(1)}, f32[256,512]{1,0:T(8,128)}, u32[]{:S(2)}) copy-start(f32[256,512]{1,0:T(8,128)} %copy-done.2) | copy-start | bytes 1572868
  171.5 4.0 %copy-start.4 = (f32[256,512]{1,0:T(8,128)S(1)}, f32[256,512]{1,0:T(8,128)}, u32[]{:S(2)}) copy-start(f32[256,512]{1,0:T(8,128)} %reduce-scatter.8.cloned.1.call-done) | copy-start | bytes 1572868
  173.3 4.8 %copy-start.12 = (f32[256]{0:T(256)S(1)}, f32[256]{0:T(256)}, u32[]{:S(2)}) copy-start(f32[256]{0:T(256)} %get-tuple-element.41) | copy-start | bytes 3076
  173.3 27.4 %copy-start.11 = (f32[1,256]{1,0:T(1,128)S(1)}, f32[1,256]{1,0:T(1,128)}, u32[]{:S(2)}) copy-start(f32[1,256]{1,0:T(1,128)} %copy-done.10) | copy-start | bytes 3076
  173.3 27.4 %copy-start.13 = (f32[512]{0:T(512)S(1)}, f32[512]{0:T(512)}, u32[]{:S(2)}) copy-start(f32[512]{0:T(512)} %param.21) | copy-start | bytes 6148
Sparse Core Ops, SparseCore 0:
  13.9 37.7 all-reduce.6
  79.2 33.4 all-reduce.8
  176.9 166.2 all-reduce.10
Sparse Core Ops, SparseCore 1:
  19.7 51.7 all-gather.1
  84.6 86.8 reduce-scatter.7
  175.0 97.7 reduce-scatter.3
  276.7 62.7 reduce-scatter.5
where the time goes:
time: 357 us; the launch traced here: 356 us
  waiting for transfers between devices  230 us (64%)
  blocking collectives  60.2 us (17%)
  matrix products  33.3 us (9%)
  between operations  17.4 us (5%)
  local copies, waits for them, and re-layouts  11.7 us (3%)
    reduce_scatter x1, waiting for transfers between devices, local(): lax.psum_scatter(grad_w_two_part, 'dp', scatter_dimension=1, tiled=True)  64.7 us
    reduce_scatter x1, waiting for transfers between devices, local(): lax.psum_scatter(contract_rows(columns, coeffs_b) * inv_scale, 'dp', scat...  51 us
    psum x1, blocking collectives, local(): loss_value = lax.psum(loss_part, ('dp', 'query')) / count_all  38.7 us
    psum x1, waiting for transfers between devices, local(): coeffs = lax.psum(partial_value, 'query') + b_two  32 us
    reduce_scatter x1, waiting for transfers between devices, local(): lax.psum_scatter(contract_rows(columns, grad_pre_b), 'dp', scatter_dimens...  31 us
    psum x1, waiting for transfers between devices, local(): lax.psum(jnp.dot(misfit_b, basis_all, preferred_element_type=jnp.float32)...  28.1 us
    psum x1, blocking collectives, local(): lax.psum((jnp.sum(grad_pre, axis=0), jnp.sum(grad_coeffs, axis=0)), 'dp')  21.5 us
    all_gather x1, waiting for transfers between devices, local(): basis_all = lax.all_gather(basis_b, 'dp', axis=0, tiled=True)  19.8 us
  transfers between devices with their start and end apart: 7, of which 7 were waited for; matrix products, arithmetic and copies ran while one was open for 8% of the time, Pallas kernels for 0%

commit v1 on v0

--- a/solution.py
+++ b/solution.py
@@ -88,7 +88,9 @@
     first_act, first_b, second_act, second_b, basis_b = trunk_forward(
         coords_mine, v_one, c_one, v_two, c_two, v_three, c_three
     )
-    basis_all = lax.all_gather(basis_b, "dp", axis=0, tiled=True)
+    basis_all = jnp.concatenate(
+        lax.all_to_all(jnp.stack([basis_b] * lax.axis_size("dp")), "dp", 0, 0), axis=0
+    )
     prediction = contract_cols(coeffs_b, basis_all) * inv_scale
     misfit = prediction - targets.astype(jnp.float32)
     loss_part = jnp.sum(misfit * misfit)

time: 357 us -> 517 us (1.45)
  waiting for transfers between devices: 230 us -> 385 us
  starting transfers between devices: 0.3 us -> 7.56 us
    psum x1, waiting for transfers between devices: 3.7 us -> 140 us  [local(): lax.psum((trunk_parts[0], trunk_parts[1], trunk_parts[2], trunk_parts[3],...]
    reduce_scatter x1, waiting for transfers between devices: 51 us -> 84.2 us  [local(): lax.psum_scatter(contract_rows(columns, coeffs_b) * inv_scale, 'dp', scat...]
    all_gather x1 -> x0, waiting for transfers between devices: 19.8 us -> none  [local(): basis_all = lax.all_gather(basis_b, 'dp', axis=0, tiled=True)]
    all_to_all x0 -> x1, waiting for transfers between devices: none -> 8.08 us  [local(): lax.all_to_all(jnp.stack([basis_b] * lax.axis_size('dp')), 'dp', 0, 0)]
    reduce_scatter x1, waiting for transfers between devices: 31 us -> 23.6 us  [local(): lax.psum_scatter(contract_rows(columns, grad_pre_b), 'dp', scatter_dimens...]
    all_to_all x0 -> x1, starting transfers between devices: none -> 7.31 us  [local(): lax.all_to_all(jnp.stack([basis_b] * lax.axis_size('dp')), 'dp', 0, 0)]
    unnamed x31 -> x29, local copies, waits for them, and re-layouts: 10.9 us -> 9.06 us
  transfers between devices with their start and end apart: 7 -> 7, of which waited for: 7 -> 7; matrix products, arithmetic and copies ran while one was open for 8% -> 5% of each run, Pallas kernels for 0% -> 0%
where the time goes in v1:
time: 517 us; the launch traced here: 516 us
  waiting for transfers between devices  385 us (74%)
  blocking collectives  58.6 us (11%)
  matrix products  34 us (7%)
  between operations  16 us (3%)
  local copies, waits for them, and re-layouts  11.4 us (2%)
  starting transfers between devices  7.56 us (1%)
    psum x1, waiting for transfers between devices, local(): lax.psum((trunk_parts[0], trunk_parts[1], trunk_parts[2], trunk_parts[3],...  140 us
    reduce_scatter x1, waiting for transfers between devices, local(): lax.psum_scatter(contract_rows(columns, coeffs_b) * inv_scale, 'dp', scat...  84.2 us
    reduce_scatter x1, waiting for transfers between devices, local(): lax.psum_scatter(grad_w_two_part, 'dp', scatter_dimension=1, tiled=True)  64 us
    psum x1, blocking collectives, local(): loss_value = lax.psum(loss_part, ('dp', 'query')) / count_all  37.1 us
    psum x1, waiting for transfers between devices, local(): coeffs = lax.psum(partial_value, 'query') + b_two  36.3 us
    psum x1, waiting for transfers between devices, local(): lax.psum(jnp.dot(misfit_b, basis_all, preferred_element_type=jnp.float32)...  28.8 us
    reduce_scatter x1, waiting for transfers between devices, local(): lax.psum_scatter(contract_rows(columns, grad_pre_b), 'dp', scatter_dimens...  23.6 us
    psum x1, blocking collectives, local(): lax.psum((jnp.sum(grad_pre, axis=0), jnp.sum(grad_coeffs, axis=0)), 'dp')  21.5 us
  transfers between devices with their start and end apart: 7, of which 7 were waited for; matrix products, arithmetic and copies ran while one was open for 5% of the time, Pallas kernels for 0%

profile of v1, /device:TPU:0, one launch (start us, length us, event | category | flops | bytes accessed | tf_op | source)
XLA Modules:
  0.0 516.0 jit_solution(6884047799347011229)
XLA Ops:
  7.2 0.8 fusion.21
  8.9 1.4 fusion
  11.1 1.4 fusion.1
  12.5 1.5 stack.2
  14.0 7.3 %all-to-all-start = ((bf16[8,256,512]{2,1,0:T(8,128)(2,1)}), bf16[8,256,512]{2,1,0:T(8,128)(2,1)}, u32[]{:S(2)}, u32[]{:S(2)}) async-start(bf16[8,256,512]{2,1,0:T(8,128)(2,1)} %stack.2), calls=%async_computation | async-start | bytes 4194304 | tf_op jit(solution)/shard_map/all_to_all | solution.py:92
  21.4 2.6 fusion.2
  24.0 1.1 fusion.19
  25.2 36.3 %all-reduce.7.cloned.1.call-done = f32[384,512]{1,0:T(8,128)} async-done(((f32[384,512]{1,0:T(8,128)}), f32[384,512]{1,0:T(8,128)}) %all-reduce.7.cloned.1.call-update) | async-done | bytes 786448 | tf_op jit(solution)/shard_map/psum | solution.py:82
  61.6 8.1 %all-to-all-done = bf16[8,256,512]{2,1,0:T(8,128)(2,1)} async-done(((bf16[8,256,512]{2,1,0:T(8,128)(2,1)}), bf16[8,256,512]{2,1,0:T(8,128)(2,1)}, u32[]{:S(2)}, u32[]{:S(2)}) %all-to-all-start) | async-done | bytes 2097184 | tf_op jit(solution)/shard_map/all_to_all | solution.py:92
  69.6 4.0 multiply_reduce_fusion
  73.7 1.7 copy-done.1
  75.3 3.4 convolution_multiply_fusion.1
  78.8 5.3 %convolution_multiply_fusion = f32[2048,512]{1,0:T(8,128)} fusion(f32[384,2048]{1,0:T(8,128)} %copy-done.1, f32[384,512]{1,0:T(8,128)} %all-reduce.7.cloned.1.call-done, f32[512]{0:T(512)S(1)} %copy-done.6), kind=kOutput, calls=%fused_computation.1 | convolution fusion | flops 808321024 | bytes 8128512 | tf_op jit(solution)/shard_map/dot_general | solution.py:11
  84.2 28.8 %all-reduce.9.cloned.1.call-done = f32[384,512]{1,0:T(8,128)} async-done(((f32[384,512]{1,0:T(8,128)}), f32[384,512]{1,0:T(8,128)}) %all-reduce.9.cloned.1.call-update) | async-done | bytes 786448 | tf_op jit(solution)/shard_map/psum | solution.py:98
  113.0 2.1 fusion.28
  115.1 3.2 convolution_bitcast_fusion
  118.4 2.3 fusion.8
  120.7 84.2 %reduce-scatter.8.cloned.1.call-done = f32[256,512]{1,0:T(8,128)} async-done(((f32[2048,512]{1,0:T(8,128)}), f32[256,512]{1,0:T(8,128)}) %reduce-scatter.8.cloned.1.call-update) | async-done | bytes 524304 | tf_op jit(solution)/shard_map/reduce_scatter | solution.py:104
  205.0 1.8 fusion.27
  206.8 2.2 fusion.4
  209.0 1.3 fusion.13
  210.3 1.2 reduce_sum.56
  211.5 21.5 %all-reduce.2 = (f32[256]{0:T(256)}, f32[512]{0:T(512)}) all-reduce(f32[256]{0:T(256)S(1)} %copy-done.11, f32[512]{0:T(512)S(1)} %reduce_sum.56), channel_id=1, replica_groups=mesh['dp'=8,'query'=4] {'dp'}, use_global_device_ids=true, to_apply=%region_6.0 | all-reduce | flops 768 | bytes 6144 | tf_op jit(solution)/shard_map/psum | solution.py:113
  233.0 1.1 reduce_sum.59
  234.1 1.4 fusion.26
  235.9 37.1 %all-reduce = (f32[]{:T(128)}, f32[2,512]{1,0:T(2,128)}, f32[512]{0:T(512)}, f32[512]{0:T(512)}, f32[512]{0:T(512)}) all-reduce(f32[]{:T(128)} %get-tuple-element.35, f32[2,512]{1,0:T(2,128)S(1)} %fusion.29, f32[512]{0:T(512)S(1)} %get-tuple-element.37, ...), channel_id=1, replica_groups=mesh['dp'=8,'query'=4] {'dp','query'}, use_global_device_ids=true, to_apply=%region_2.0 | all-reduce | flops 2561 | bytes 20488 | tf_op jit(solution)/shard_map/psum | solution.py:102
  273.6 23.6 %reduce-scatter.4.cloned.1.call-done = f32[512,256]{0,1:T(8,128)} async-done(((f32[4096,256]{0,1:T(8,128)}), f32[512,256]{0,1:T(8,128)}) %reduce-scatter.4.cloned.1.call-update) | async-done | bytes 524304 | tf_op jit(solution)/shard_map/reduce_scatter | solution.py:117
  297.2 2.0 copy.24
  299.3 64.0 %reduce-scatter.6.cloned.1.call-done = f32[256,64]{0,1:T(8,128)} async-done(((f32[256,512]{0,1:T(8,128)}), f32[256,64]{0,1:T(8,128)}) %reduce-scatter.6.cloned.1.call-update) | async-done | bytes 65552 | tf_op jit(solution)/shard_map/reduce_scatter | solution.py:120
  363.2 140.2 %all-reduce.11.cloned.1.call-done = (f32[512,512]{1,0:T(8,128)}, f32[512,512]{1,0:T(8,128)}) async-done(((f32[512,512]{1,0:T(8,128)}, f32[512,512]{1,0:T(8,128)}), (f32[512,512]{1,0:T(8,128)}, f32[512,512]{1,0:T(8,128)})) %all-reduce.11.cloned.1.call-update) | async-done | bytes 2097168 | tf_op jit(solution)/shard_map/psum | solution.py:121
  503.5 2.3 copy.29
  505.7 2.3 copy.30
  (40 shorter events, 2.4 us)
Async XLA Ops:
  7.2 14.2 %copy-start = (bf16[384,4096]{1,0:T(8,128)(2,1)S(1)}, bf16[384,4096]{1,0:T(8,128)(2,1)}, u32[]{:S(2)}) copy-start(bf16[384,4096]{1,0:T(8,128)(2,1)} %param.13) | copy-start | bytes 9437188
  8.0 0.8 copy-start.7
  8.0 2.3 copy-start.9
  10.3 0.8 copy-start.2
  14.0 55.6 %all-to-all-start = ((bf16[8,256,512]{2,1,0:T(8,128)(2,1)}), bf16[8,256,512]{2,1,0:T(8,128)(2,1)}, u32[]{:S(2)}, u32[]{:S(2)}) async-start(bf16[8,256,512]{2,1,0:T(8,128)(2,1)} %stack.2), calls=%async_computation | async-start | bytes 4194304 | tf_op jit(solution)/shard_map/all_to_all | solution.py:92
  21.3 48.3 %copy-start.6 = (f32[512]{0:T(512)S(1)}, f32[512]{0:T(512)}, u32[]{:S(2)}) copy-start(f32[512]{0:T(512)} %param.19) | copy-start | bytes 6148
  21.3 40.3 %all-reduce.7.cloned.1.call-start = ((), (), s32[]{:S(2)}) async-start(), calls=%async_computation.4 | async-start | bytes 1572864 | tf_op jit(solution)/shard_map/psum | solution.py:82
  21.4 2.6 copy-start.5
  25.2 87.8 %all-reduce.9.cloned.1.call-start = ((), (), s32[]{:S(2)}) async-start(), calls=%async_computation.5 | async-start | bytes 1572864 | tf_op jit(solution)/shard_map/psum | solution.py:98
  73.7 1.7 copy-start.1
  78.8 126.2 %reduce-scatter.8.cloned.1.call-start = ((), (), s32[]{:S(2)}) async-start(), calls=%async_computation.8 | async-start | bytes 4718592 | tf_op jit(solution)/shard_map/reduce_scatter | solution.py:104
  84.2 213.0 %reduce-scatter.4.cloned.1.call-start = ((), (), s32[]{:S(2)}) async-start(), calls=%async_computation.6 | async-start | bytes 4718592 | tf_op jit(solution)/shard_map/reduce_scatter | solution.py:117
  118.3 88.5 %copy-start.8 = (f32[1,256]{1,0:T(1,128)S(1)}, f32[1,256]{1,0:T(1,128)}, u32[]{:S(2)}) copy-start(f32[1,256]{1,0:T(1,128)} %copy-done.7) | copy-start | bytes 3076
  118.3 244.9 %reduce-scatter.6.cloned.1.call-start = ((), (), s32[]{:S(2)}) async-start(), calls=%async_computation.7 | async-start | bytes 589824 | tf_op jit(solution)/shard_map/reduce_scatter | solution.py:120
  120.7 382.8 %all-reduce.11.cloned.1.call-start = ((), (), s32[]{:S(2)}) async-start(), calls=%async_computation.9 | async-start | bytes 4194304 | tf_op jit(solution)/shard_map/psum | solution.py:121
  205.0 4.0 copy-start.3
  205.0 4.0 copy-start.4
  206.8 4.8 copy-start.11
  206.8 27.3 %copy-start.10 = (f32[1,256]{1,0:T(1,128)S(1)}, f32[1,256]{1,0:T(1,128)}, u32[]{:S(2)}) copy-start(f32[1,256]{1,0:T(1,128)} %copy-done.9) | copy-start | bytes 3076
  206.8 27.3 %copy-start.12 = (f32[512]{0:T(512)S(1)}, f32[512]{0:T(512)}, u32[]{:S(2)}) copy-start(f32[512]{0:T(512)} %param.21) | copy-start | bytes 6148
Sparse Core Ops, SparseCore 0:
  25.3 36.2 all-reduce.6
  78.9 34.0 all-reduce.8
  116.6 88.2 reduce-scatter.7
  208.4 88.7 reduce-scatter.3
  301.0 62.2 reduce-scatter.5
  369.8 133.6 all-reduce.10
